TPU v7x, 32 devices: a whole 2x2x4 slice. The times are simulated.
32 devices in a mesh: orb: 4 (over y, x), aux: 8 (over z, core).
Axes of the slice: x: 2, y: 2, z: 4, core: 2. Of those that a mesh axis runs over, the one named last changes fastest.
Arguments:
- raw_rows: bfloat16 [128, 1024, 128], P('orb', 'aux'), may hold values from -4 to 4
- fit_metric: bfloat16 [128, 512, 512], P(('orb', 'aux'))
- domain: int32 [128, 512], P('orb'), may hold values from 0 to 127, as said below
- counts: int32 [128, 8], P('orb'), may hold values from 32 to 128, as said below
- orbital_ids: int32 [128], P(('orb', 'aux')), may hold values from 0 to 127, each once
- occ_energy: float32 [128], replicated, may hold values from -1.5 to -0.3
- osv_energy: bfloat16 [128, 128], P(('orb', 'aux')), may hold values from 0.29882812 to 3
- matchings: int32 [4, 4], replicated, may hold values from 0 to 3, as said below
- screening: int32 [128, 5, 4], P(('orb', 'aux')), may hold values 0 or 1
Outputs:
- density: float32 [128, 1024, 128], P('orb', 'aux')
- pair_energy: float32 [128, 5, 4], P(('orb', 'aux'))
Inputs may be any that keep to these rules, and one draw needn't show every extreme that they name: `counts`: every row sums to 512; every entry is at most 128, and every row has an entry equal to 128. `domain`: the positions of a row are taken by owner 0 first, then owner 1 and so on, in the numbers that counts gives; within one owner's run the entries are distinct. `matchings`: row q maps orb index o to o XOR m_q, with a mask m_q from 1 to 3; rounds may repeat a mask.
All inputs are finite; a program needn't handle non-finite values. No bound on the sum of `screening` on one device may be relied on, other than what follows from the above.
Results may differ from a plain program's by a relative error of at most 0.0029.
Values may be sent and summed in bfloat16 or wider, within the bound.
A program may use at most 128 MiB of HBM per device.

v0:
```python
import jax
import jax.numpy as jnp
from jax import lax
from jax.sharding import PartitionSpec as P

PAIR_SCALE = 1.3


def lookup_energy(identities, energy_table):
    everyone = jnp.arange(energy_table.shape[0], dtype=jnp.int32)
    return jnp.sum(
        jnp.where(identities[:, None] == everyone[None, :], energy_table[None, :], 0.0), axis=1
    )


def pair_terms(density, raw_full, own_occ, own_osv, partner_block, occ_energy, screen_round):
    far_fitted, far_rows, far_osv, far_names = partner_block
    orbitals, aux_total, osv_count = raw_full.shape
    far_occ = lookup_energy(far_names, occ_energy)
    spread_out = jnp.zeros((orbitals, aux_total, osv_count), jnp.bfloat16)
    spread_out = spread_out.at[jnp.arange(orbitals, dtype=jnp.int32)[:, None], far_rows].set(
        far_fitted
    )
    integrals = jnp.einsum(
        "kpa,lpb->klab", raw_full, spread_out, preferred_element_type=jnp.float32
    )
    denominator = (
        own_osv[:, None, :, None]
        + far_osv.astype(jnp.float32)[None, :, None, :]
        - own_occ[:, None, None, None]
        - far_occ[None, :, None, None]
    )
    amplitudes = (screen_round[:, :, None, None] * integrals / denominator).astype(jnp.bfloat16)
    widened = lax.optimization_barrier(amplitudes).astype(jnp.float32)
    energy = PAIR_SCALE * jnp.sum(widened * integrals, axis=(2, 3)) / (osv_count * osv_count)
    density = density + jnp.einsum(
        "klab,lpb->kpa", amplitudes, spread_out, preferred_element_type=jnp.float32
    )
    return (density, energy)


def per_device(
    raw_rows, fit_metric, domain, counts, orbital_ids, occ_energy, osv_energy, matchings, screening
):
    aux_count = lax.axis_size("aux")
    my_aux = lax.axis_index("aux")
    my_orb = lax.axis_index("orb")
    group_slots, aux_dev, osv_count = raw_rows.shape
    fit_count = domain.shape[1]
    orbitals = group_slots // aux_count
    capacity = 2 * fit_count // aux_count
    aux_total = aux_dev * aux_count
    run_ends = jnp.cumsum(counts, axis=1)
    run_starts = run_ends - counts
    slot_index = jnp.arange(capacity, dtype=jnp.int32)
    send_start = lax.dynamic_index_in_dim(run_starts, my_aux, 1, keepdims=False)
    send_count = lax.dynamic_index_in_dim(counts, my_aux, 1, keepdims=False)
    is_valid = slot_index[None, :] < send_count[:, None]
    where_at = jnp.minimum(send_start[:, None] + slot_index[None, :], fit_count - 1)
    local_rows = jnp.where(is_valid, jnp.take_along_axis(domain, where_at, axis=1), 0)
    flat_index = jnp.arange(group_slots, dtype=jnp.int32)[:, None] * aux_dev + local_rows
    packed = jnp.take(raw_rows.reshape(group_slots * aux_dev, osv_count), flat_index, axis=0)
    packed = jnp.where(is_valid[:, :, None], packed, jnp.zeros((), jnp.bfloat16))
    packed = packed.reshape(aux_count, orbitals, capacity, osv_count)
    received = lax.all_to_all(packed, "aux", split_axis=0, concat_axis=0, tiled=True)
    own_counts = lax.dynamic_slice_in_dim(counts, my_aux * orbitals, orbitals, 0)
    own_domain = lax.dynamic_slice_in_dim(domain, my_aux * orbitals, orbitals, 0)
    own_ends = jnp.cumsum(own_counts, axis=1)
    own_starts = own_ends - own_counts
    positions = jnp.arange(fit_count, dtype=jnp.int32)
    source = jnp.sum((positions[None, :, None] >= own_ends[:, None, :]).astype(jnp.int32), axis=2)
    offset = positions[None, :] - jnp.take_along_axis(own_starts, source, axis=1)
    local_range = jnp.arange(orbitals, dtype=jnp.int32)
    gather_index = (source * orbitals + local_range[:, None]) * capacity + offset
    gathered_rows = jnp.take(
        received.reshape(aux_count * orbitals * capacity, osv_count), gather_index, axis=0
    )
    rows_global = source * aux_dev + own_domain
    fitted = jnp.einsum(
        "kpq,kqa->kpa", fit_metric, gathered_rows, preferred_element_type=jnp.float32
    ).astype(jnp.bfloat16)
    raw_full = jnp.zeros((orbitals, aux_total, osv_count), jnp.bfloat16)
    raw_full = raw_full.at[local_range[:, None], rows_global].set(gathered_rows)
    own_occ = lookup_energy(orbital_ids, occ_energy)
    own_osv = osv_energy.astype(jnp.float32)
    screen_all = screening.astype(jnp.float32)
    own_block = (fitted, rows_global, osv_energy, orbital_ids)
    density = jnp.zeros((orbitals, aux_total, osv_count), jnp.float32)
    density, energy = pair_terms(
        density, raw_full, own_occ, own_osv, own_block, occ_energy, screen_all[:, 0]
    )
    energies = [energy]
    matches = matchings.shape[0]
    everyone = (
        lax.all_gather(fitted, "orb", axis=0, tiled=True),
        lax.all_gather(rows_global, "orb", axis=0, tiled=True),
        lax.all_gather(osv_energy, "orb", axis=0, tiled=True),
        lax.all_gather(orbital_ids, "orb", axis=0, tiled=True),
    )
    for round_index in range(matches):
        partner_orb = lax.dynamic_index_in_dim(matchings[round_index], my_orb, 0, keepdims=False)
        partner_block = tuple(
            (
                lax.dynamic_slice_in_dim(member, partner_orb * orbitals, orbitals, 0)
                for member in everyone
            )
        )
        density, energy = pair_terms(
            density,
            raw_full,
            own_occ,
            own_osv,
            partner_block,
            occ_energy,
            screen_all[:, round_index + 1],
        )
        energies.append(energy)
    returned = lax.all_to_all(density, "aux", split_axis=1, concat_axis=0, tiled=True)
    return (returned, jnp.stack(energies, axis=1))


def solution(mesh):
    placed = (
        P("orb", "aux", None),
        P(("orb", "aux"), None, None),
        P("orb", None),
        P("orb", None),
        P(("orb", "aux")),
        P(),
        P(("orb", "aux"), None),
        P(),
        P(("orb", "aux"), None, None),
    )
    return jax.shard_map(
        per_device,
        mesh=mesh,
        in_specs=placed,
        out_specs=(P("orb", "aux", None), P(("orb", "aux"), None, None)),
        check_vma=False,
    )
```

profile of v0, /device:TPU:25, one launch (start us, length us, event | category | flops | bytes accessed | tf_op | source)
XLA Modules:
  0.0 273.3 jit_solution(15455512390270858755)
XLA Ops:
  9.7 32.8 %gather_fusion.3 = s32[4096]{0:T(1024)S(1)} fusion(s32[32,512]{1,0:T(8,128)S(1)} %copy-done.1, s32[4096]{0:T(1024)S(1)} %or_bitcast_fusion), kind=kCustom, calls=%fused_computation.3 | custom fusion | bytes 65536 | tf_op jit(solution)/shard_map/jit(take_along_axis)/gather | solution.py:60
  42.6 15.0 %gather_fusion = bf16[4096,128]{1,0:T(8,128)(2,1)} fusion(bf16[4096,128]{1,0:T(8,128)(2,1)S(1)} %bitcast.218, s32[4096]{0:T(1024)S(1)} %fusion.15), kind=kCustom, calls=%fused_computation | custom fusion | bytes 2113536 | tf_op jit(solution)/shard_map/jit(_take)/gather | solution.py:62
  57.7 4.0 %select_select_fusion = bf16[8,4,128,128]{3,2,1,0:T(8,128)(2,1)} fusion(bf16[8,4,128,128]{3,2,1,0:T(8,128)(2,1)} %bitcast.233, pred[8,4,128]{2,1,0:T(4,128)(4,1)S(1)} %get-tuple-element.45, pred[8,4,128]{2,1,0:T(4,128)(4,1)S(1)} %get-tuple-element.44), kind=kLoop, calls=%fused_computation.32 | loop fusion | flops 1048576 | bytes 2105344 | tf_op jit(solution)/shard_map/jit(_where)/select_n | solution.py:63
  61.7 5.4 %all-to-all-start = ((bf16[8,4,128,128]{3,2,1,0:T(8,128)(2,1)}), bf16[8,4,128,128]{3,2,1,0:T(8,128)(2,1)S(1)}, u32[]{:S(2)}, u32[]{:S(2)}) async-start(bf16[8,4,128,128]{3,2,1,0:T(8,128)(2,1)} %select_select_fusion), calls=%async_computation | async-start | bytes 2097152 | tf_op jit(solution)/shard_map/all_to_all | solution.py:65
  67.5 9.0 %gather_fusion.2 = s32[2048]{0:T(1024)S(1)} fusion(s32[4,8]{0,1:T(8,128)S(1)} %fusion.72, s32[2048]{0:T(1024)S(1)} %bitcast.217), kind=kCustom, calls=%fused_computation.2 | custom fusion | bytes 32768 | tf_op jit(solution)/shard_map/jit(take_along_axis)/gather | solution.py:72
  76.6 14.5 %all-to-all-done = bf16[8,4,128,128]{3,2,1,0:T(8,128)(2,1)S(1)} async-done(((bf16[8,4,128,128]{3,2,1,0:T(8,128)(2,1)}), bf16[8,4,128,128]{3,2,1,0:T(8,128)(2,1)S(1)}, u32[]{:S(2)}, u32[]{:S(2)}) %all-to-all-start) | async-done | bytes 1048608 | tf_op jit(solution)/shard_map/all_to_all | solution.py:65
  91.1 8.0 %gather_fusion.1 = bf16[2048,128]{1,0:T(8,128)(2,1)} fusion(bf16[4096,128]{1,0:T(8,128)(2,1)S(1)} %bitcast.219, s32[2048]{0:T(1024)S(1)} %broadcast_clamp_fusion), kind=kCustom, calls=%fused_computation.1 | custom fusion | bytes 1056768 | tf_op jit(solution)/shard_map/jit(_take)/gather | solution.py:75
  104.0 5.4 %all-reduce = s32[16]{0:T(128)S(1)} all-reduce(s32[16]{0:T(128)S(1)} %dynamic-update-slice), channel_id=1, replica_groups=mesh['orb'=4,'aux'=8] {'orb'}, use_global_device_ids=true, to_apply=%add | all-reduce | flops 16 | bytes 128
  115.8 6.5 %all-gather = s32[4,4,512]{2,1,0:T(4,128)S(1)} all-gather(s32[1,4,512]{2,1,0:T(4,128)S(1)} %get-tuple-element.30), channel_id=1, replica_groups=mesh['orb'=4,'aux'=8] {'orb'}, dimensions={0}, use_global_device_ids=true | all-gather | bytes 40960 | tf_op jit(solution)/shard_map/all_gather | solution.py:96
  125.9 6.0 %all-gather.1 = bf16[4,4,128]{2,1,0:T(4,128)(2,1)S(1)} all-gather(bf16[1,4,128]{2,1,0:T(4,128)(2,1)S(1)} %bitcast.253), channel_id=1, replica_groups=mesh['orb'=4,'aux'=8] {'orb'}, dimensions={0}, use_global_device_ids=true | all-gather | bytes 5120 | tf_op jit(solution)/shard_map/all_gather | solution.py:97
  132.2 7.1 %scatter_custom_fusion = bf16[4096,128]{1,0:T(8,128)(2,1)} fusion(s32[2048]{0:T(1024)S(1)} %bitcast.251, bf16[2048,128]{1,0:T(8,128)(2,1)} %bitcast.236, bf16[]{:T(256)} %constant.113.clone.1), kind=kCustom, calls=%fused_computation.43 | custom fusion | bytes 1049088
  139.3 6.4 %scatter_custom_fusion.1 = bf16[4096,128]{1,0:T(8,128)(2,1)S(1)} fusion(s32[2048]{0:T(1024)S(1)} %bitcast.252, bf16[2048,128]{1,0:T(8,128)(2,1)} %bitcast.237, bf16[]{:T(256)} %constant.113.clone.1), kind=kCustom, calls=%fused_computation.41 | custom fusion | bytes 1049088
  145.7 2.9 %convolution_bitcast_fusion.4 = f32[4,4,128,128]{2,3,0,1:T(8,128)} fusion(bf16[4,1024,128,1]{2,1,3,0:T(8,128)(2,1)} %bitcast.227, bf16[4,1024,128,1]{2,1,0,3:T(8,128)(2,1)S(1)} %bitcast.220), kind=kOutput, calls=%fused_computation.19 | convolution fusion | flops 536870912 | bytes 3145728 | tf_op jit(solution)/shard_map/kpa,lpb->klab/dot_general | solution.py:24
  151.6 7.2 %scatter_custom_fusion.4 = bf16[4096,128]{1,0:T(8,128)(2,1)} fusion(s32[2048]{0:T(1024)S(1)} %bitcast.247, bf16[2048,128]{1,0:T(8,128)(2,1)} %bitcast.243, bf16[]{:T(256)} %constant.113.clone.1), kind=kCustom, calls=%fused_computation.35 | custom fusion | bytes 1049088
  158.7 2.9 %convolution_bitcast_fusion.1 = f32[4,4,128,128]{2,3,0,1:T(8,128)} fusion(bf16[4,1024,128,1]{2,1,3,0:T(8,128)(2,1)} %bitcast.225, bf16[4,1024,128,1]{2,1,0,3:T(8,128)(2,1)S(1)} %bitcast.221), kind=kOutput, calls=%fused_computation.16 | convolution fusion | flops 536870912 | bytes 3145728 | tf_op jit(solution)/shard_map/kpa,lpb->klab/dot_general | solution.py:24
  161.7 7.2 %scatter_custom_fusion.3 = bf16[4096,128]{1,0:T(8,128)(2,1)} fusion(s32[2048]{0:T(1024)S(1)} %bitcast.248, bf16[2048,128]{1,0:T(8,128)(2,1)} %bitcast.242, bf16[]{:T(256)} %constant.113.clone.1), kind=kCustom, calls=%fused_computation.37 | custom fusion | bytes 1049088
  168.9 2.9 %convolution_bitcast_fusion.2 = f32[4,4,128,128]{2,3,0,1:T(8,128)} fusion(bf16[4,1024,128,1]{2,1,3,0:T(8,128)(2,1)} %bitcast.229, bf16[4,1024,128,1]{2,1,0,3:T(8,128)(2,1)S(1)} %bitcast.222), kind=kOutput, calls=%fused_computation.17 | convolution fusion | flops 536870912 | bytes 3145728 | tf_op jit(solution)/shard_map/kpa,lpb->klab/dot_general | solution.py:24
  171.8 7.2 %scatter_custom_fusion.5 = bf16[4096,128]{1,0:T(8,128)(2,1)} fusion(s32[2048]{0:T(1024)S(1)} %bitcast.249, bf16[2048,128]{1,0:T(8,128)(2,1)} %bitcast.241, bf16[]{:T(256)} %constant.113.clone.1), kind=kCustom, calls=%fused_computation.33 | custom fusion | bytes 1049088
  179.0 5.1 %divide_convert_fusion = (bf16[4,4,128,128]{2,3,0,1:T(8,128)(2,1)}, bf16[4,4,128,128]{2,3,0,1:T(8,128)(2,1)}, bf16[4,4,128,128]{2,3,0,1:T(8,128)(2,1)}, bf16[4,4...) fusion(f32[4]{0:T(128)S(1)} %get-tuple-element.20, f32[4,128]{1,0:T(4,128)S(1)} %get-tuple-element.40, ...), kind=kOutput, calls=%fused_computation.27 | convolution fusion | flops 543162368 | bytes 8397120 | tf_op jit(solution)/shard_map/kpa,lpb->klab/dot_general | solution.py:24
  186.1 7.2 %scatter_custom_fusion.2 = bf16[4096,128]{1,0:T(8,128)(2,1)} fusion(s32[2048]{0:T(1024)S(1)} %bitcast.250, bf16[2048,128]{1,0:T(8,128)(2,1)} %bitcast.240, bf16[]{:T(256)} %constant.113.clone.1), kind=kCustom, calls=%fused_computation.39 | custom fusion | bytes 1049088
  193.3 3.1 %divide_convert_fusion.3 = (bf16[4,4,128,128]{2,3,0,1:T(8,128)(2,1)S(1)}, f32[4,4,128,128]{2,3,0,1:T(8,128)}) fusion(f32[4]{0:T(128)S(1)} %get-tuple-element.21, f32[4,128]{1,0:T(4,128)S(1)} %get-tuple-element.43, f32[4,4]{0,1:T(4,128)S(1)} %bitcast.254, f32[4]{0:T(128)S(1)} %get-tuple-element.24, f32[4,128]{1,0:T(4,128)S(1)} %convert_element_type.62, ...), kind=kOutput, calls=%fused_computation.30 | convolution fusion | flops 538443776 | bytes 3674208 | tf_op jit(solution)/shard_map/kpa,lpb->klab/dot_general | solution.py:24
  204.9 11.9 %all-to-all-start.1 = ((f32[4,1024,128]{2,0,1:T(4,128)}), f32[4,1024,128]{2,0,1:T(4,128)}, u32[]{:S(2)}, u32[]{:S(2)}) async-start(f32[4,1024,128]{2,0,1:T(4,128)} %copy.100), calls=%async_computation.1 | async-start | bytes 4194304 | tf_op jit(solution)/shard_map/all_to_all | solution.py:118
  225.3 37.9 %all-to-all-done.1 = f32[4,1024,128]{2,0,1:T(4,128)} async-done(((f32[4,1024,128]{2,0,1:T(4,128)}), f32[4,1024,128]{2,0,1:T(4,128)}, u32[]{:S(2)}, u32[]{:S(2)}) %all-to-all-start.1) | async-done | bytes 2097184 | tf_op jit(solution)/shard_map/all_to_all | solution.py:118
  263.2 3.2 %copy.101 = f32[8,4,128,128]{3,2,1,0:T(8,128)} copy(f32[8,4,128,128]{3,1,2,0:T(4,128)} %bitcast.71) | data formatting | bytes 4194304 | tf_op jit(solution)/shard_map/all_to_all | solution.py:118
  (142 shorter events, 31.8 us)
Async XLA Ops:
  7.2 93.4 %copy-start = (bf16[4,512,512]{2,1,0:T(8,128)(2,1)S(1)}, bf16[4,512,512]{2,1,0:T(8,128)(2,1)}, u32[]{:S(2)}) copy-start(bf16[4,512,512]{2,1,0:T(8,128)(2,1)} %param.10) | copy-start | bytes 6291460
  7.2 2.5 copy-start.1
  9.7 32.9 %copy-start.2 = (bf16[32,128,128]{2,1,0:T(8,128)(2,1)S(1)}, bf16[32,128,128]{2,1,0:T(8,128)(2,1)}, u32[]{:S(2)}) copy-start(bf16[32,128,128]{2,1,0:T(8,128)(2,1)} %param.9) | copy-start | bytes 3145732
  57.7 9.4 %copy-start.17 = (s32[32,8]{0,1:T(8,128)S(1)}, s32[32,8]{0,1:T(8,128)}, u32[]{:S(2)}) copy-start(s32[32,8]{0,1:T(8,128)} %param.12) | copy-start | bytes 3076
  61.7 29.4 %all-to-all-start = ((bf16[8,4,128,128]{3,2,1,0:T(8,128)(2,1)}), bf16[8,4,128,128]{3,2,1,0:T(8,128)(2,1)S(1)}, u32[]{:S(2)}, u32[]{:S(2)}) async-start(bf16[8,4,128,128]{3,2,1,0:T(8,128)(2,1)} %select_select_fusion), calls=%async_computation | async-start | bytes 2097152 | tf_op jit(solution)/shard_map/all_to_all | solution.py:65
  67.1 81.5 %all-gather.4.cloned.1.call-start = ((), (), s32[]{:S(2)}) async-start(), calls=%async_computation.2 | async-start | bytes 2621440 | tf_op jit(solution)/shard_map/all_gather | solution.py:95
  100.5 1.9 copy-start.10
  100.6 2.0 copy-start.25
  100.6 3.2 %copy-start.23 = (s32[4]{0:T(128)S(1)}, s32[4]{0:T(128)}, u32[]{:S(2)}) copy-start(s32[4]{0:T(128)} %param.13) | copy-start | bytes 52
  100.6 8.8 %copy-start.20 = (s32[4,4]{1,0:T(4,128)S(1)}, s32[4,4]{1,0:T(4,128)}, u32[]{:S(2)}) copy-start(s32[4,4]{1,0:T(4,128)} %param.16) | copy-start | bytes 196
  100.6 24.3 %copy-start.22 = (s32[2]{0:T(128)S(1)}, s32[2]{0:T(128)}, u32[]{:S(2)}) copy-start(s32[2]{0:T(128)} %constant.137) | copy-start | bytes 28
  100.6 24.3 %copy-start.21 = (s32[2]{0:T(128)S(1)}, s32[2]{0:T(128)}, u32[]{:S(2)}) copy-start(s32[2]{0:T(128)} %constant.140) | copy-start | bytes 28
  100.6 24.6 %copy-start.18 = (s32[4,5,4]{1,2,0:T(4,128)S(1)}, s32[4,5,4]{1,2,0:T(4,128)}, u32[]{:S(2)}) copy-start(s32[4,5,4]{1,2,0:T(4,128)} %param.17) | copy-start | bytes 964
  100.6 25.1 %copy-start.19 = (bf16[4,128]{1,0:T(4,128)(2,1)S(1)}, bf16[4,128]{1,0:T(4,128)(2,1)}, u32[]{:S(2)}) copy-start(bf16[4,128]{1,0:T(4,128)(2,1)} %param.15) | copy-start | bytes 3076
  100.6 31.3 %copy-start.24 = (f32[128]{0:T(128)S(1)}, f32[128]{0:T(128)}, u32[]{:S(2)}) copy-start(f32[128]{0:T(128)} %param.14) | copy-start | bytes 1540
  179.0 5.1 %copy-start.6 = (bf16[4096,128]{1,0:T(8,128)(2,1)S(1)}, bf16[4096,128]{1,0:T(8,128)(2,1)}, u32[]{:S(2)}) copy-start(bf16[4096,128]{1,0:T(8,128)(2,1)} %scatter_custom_fusion) | copy-start | bytes 3145732
  184.0 2.0 copy-start.15
  193.3 3.1 %copy-start.12 = (bf16[4096,128]{1,0:T(8,128)(2,1)S(1)}, bf16[4096,128]{1,0:T(8,128)(2,1)}, u32[]{:S(2)}) copy-start(bf16[4096,128]{1,0:T(8,128)(2,1)} %scatter_custom_fusion.2) | copy-start | bytes 3145732
  196.4 1.4 copy-start.7
  196.4 1.5 copy-start.14
  199.3 2.1 copy-start.11
  204.9 58.4 %all-to-all-start.1 = ((f32[4,1024,128]{2,0,1:T(4,128)}), f32[4,1024,128]{2,0,1:T(4,128)}, u32[]{:S(2)}, u32[]{:S(2)}) async-start(f32[4,1024,128]{2,0,1:T(4,128)} %copy.100), calls=%async_computation.1 | async-start | bytes 4194304 | tf_op jit(solution)/shard_map/all_to_all | solution.py:118
  216.7 3.4 %copy-start.3 = (f32[4,4,128,128]{2,3,0,1:T(8,128)S(1)}, f32[4,4,128,128]{2,3,0,1:T(8,128)}, u32[]{:S(2)}) copy-start(f32[4,4,128,128]{2,3,0,1:T(8,128)} %convolution_bitcast_fusion.4) | copy-start | bytes 3145732
  221.4 1.8 copy-start.4
  (5 other events, 6.0 us)
Sparse Core Ops, SparseCore 0:
  102.6 35.7 all-gather.3
where the time goes:
time: 278 us; the launch traced here: 273 us
  local copies, waits for them, and re-layouts  124 us (45%)
  waiting for transfers between devices  52.4 us (19%)
  between operations  22.8 us (8%)
  matrix products  22.7 us (8%)
  blocking collectives  17.8 us (6%)
  starting transfers between devices  17.2 us (6%)
  other arithmetic  16.7 us (6%)
    unnamed x74, local copies, waits for them, and re-layouts  46.9 us
    all_to_all x1, waiting for transfers between devices, per_device(): lax.all_to_all(density, 'aux', split_axis=1, concat_axis=0, tiled=True)  37.9 us
    gather x1, local copies, waits for them, and re-layouts, per_device(): jnp.take_along_axis(domain, where_at, axis=1)  32.8 us
    dot_general x5, matrix products, pair_terms(): jnp.einsum('kpa,lpb->klab', raw_full, spread_out, preferred_element_type=...  16.9 us
    gather x1, local copies, waits for them, and re-layouts, per_device(): jnp.take(raw_rows.reshape(group_slots * aux_dev, osv_count), flat_index,...  15 us
    all_to_all x1, waiting for transfers between devices, per_device(): lax.all_to_all(packed, 'aux', split_axis=0, concat_axis=0, tiled=True)  14.5 us
    all_to_all x1, starting transfers between devices, per_device(): lax.all_to_all(density, 'aux', split_axis=1, concat_axis=0, tiled=True)  11.9 us
    gather x3, local copies, waits for them, and re-layouts, per_device(): jnp.take_along_axis(own_starts, source, axis=1)  8.98 us
  transfers between devices with their start and end apart: 3, of which 2 were waited for; matrix products, arithmetic and copies ran while one was open for 14% of the time, Pallas kernels for 0%

commit v1 on v0

v1 whole, which is shorter than its diff:
```python
import functools

import jax
import jax.numpy as jnp
from jax import lax
from jax.experimental import pallas as pl
from jax.experimental.pallas import tpu as pltpu
from jax.sharding import PartitionSpec as P

PAIR_SCALE = 1.3
MESH = pl.DeviceIdType.MESH
NT = (((1,), (1,)), ((), ()))


def kernel(
    n_orb,
    n_aux,
    raw_ref,
    metric_ref,
    domain_ref,
    counts_ref,
    ids_ref,
    occ_ref,
    osv_ref,
    match_ref,
    screen_ref,
    out_ref,
    energy_ref,
    raw_full,
    metric,
    st_own,
    st_far,
    ms,
    mask,
    rt,
    fitted,
    rows,
    levels,
    level_col,
    grid_full,
    integrals,
    amps,
    outgoing,
    raw_send,
    raw_recv,
    fit_send,
    fit_recv,
    meta_send,
    meta_recv,
    den_send,
    den_recv,
    local_sem,
):
    occ, fit = metric_ref.shape[0], metric_ref.shape[1]
    aux_dev, osv = raw_ref.shape[2], raw_ref.shape[3]
    aux_total = n_aux * aux_dev
    matches = match_ref.shape[0] // n_orb
    my_orb = lax.axis_index("orb")
    me = lax.axis_index("aux")

    def aux_peer(step):
        return lax.rem(me + step, n_aux)

    def orb_peer(step):
        return lax.rem(my_orb + step, n_orb)

    barrier = pltpu.get_barrier_semaphore()
    for step in range(1, n_aux):
        pl.semaphore_signal(barrier, inc=1, device_id=(my_orb, aux_peer(step)), device_id_type=MESH)
    for step in range(1, n_orb):
        pl.semaphore_signal(barrier, inc=1, device_id=(orb_peer(step), me), device_id_type=MESH)

    metric_copy = pltpu.make_async_copy(metric_ref, metric, local_sem.at[0])
    metric_copy.start()
    own_raw = pltpu.make_async_copy(raw_ref.at[me], raw_full.at[:, me], local_sem.at[1])
    own_raw.start()
    pl.semaphore_wait(barrier, n_aux + n_orb - 2)

    def raw_copy(k, step):
        return pltpu.make_async_remote_copy(
            src_ref=raw_ref.at[aux_peer(step), k],
            dst_ref=raw_full.at[k, me],
            send_sem=raw_send.at[k, step],
            recv_sem=raw_recv.at[k, step],
            device_id=(my_orb, aux_peer(step)),
            device_id_type=MESH,
        )

    def fit_copy(k, step):
        return pltpu.make_async_remote_copy(
            src_ref=fitted.at[k, 0],
            dst_ref=fitted.at[k, step],
            send_sem=fit_send.at[k, step],
            recv_sem=fit_recv.at[k, step],
            device_id=(orb_peer(step), me),
            device_id_type=MESH,
        )

    def meta_copy(which, ref, step):
        return pltpu.make_async_remote_copy(
            src_ref=ref.at[0],
            dst_ref=ref.at[step],
            send_sem=meta_send.at[which, step],
            recv_sem=meta_recv.at[which, step],
            device_id=(orb_peer(step), me),
            device_id_type=MESH,
        )

    def den_copy(owner):
        return pltpu.make_async_remote_copy(
            src_ref=outgoing.at[owner],
            dst_ref=out_ref.at[me],
            send_sem=den_send.at[owner],
            recv_sem=den_recv.at[lax.rem(me - owner + n_aux, n_aux)],
            device_id=(my_orb, owner),
            device_id_type=MESH,
        )

    def send_raw(k, carry):
        def one(step, inner):
            raw_copy(k, step).start()
            return inner

        return lax.fori_loop(1, n_aux, one, carry)

    lax.fori_loop(0, occ, send_raw, 0)

    positions = lax.broadcasted_iota(jnp.int32, (1, fit), 1)
    for k in range(occ):
        end = jnp.int32(0)
        owner = jnp.zeros((1, fit), jnp.int32)
        for j in range(n_aux):
            end = end + counts_ref[(me * occ + k) * n_aux + j]
            owner = owner + jnp.where(positions >= end, 1, 0)
        rows[0, k : k + 1, :] = owner * aux_dev + domain_ref[me, k : k + 1, :]
        level = osv_ref[k : k + 1, :].astype(jnp.float32) - occ_ref[ids_ref[k]]
        levels[0, k : k + 1, :] = level
        level_col[k * osv : (k + 1) * osv, :] = jnp.broadcast_to(level, (osv, osv)).T
    for step in range(1, n_orb):
        meta_copy(0, rows, step).start()
        meta_copy(1, levels, step).start()

    def place(row, target):
        height = 128
        base = lax.broadcasted_iota(jnp.int32, (height, fit), 0)
        for j in range(aux_total // height):
            target[j * height : (j + 1) * height, :] = jnp.where(
                base == row - j * height, 1.0, 0.0
            ).astype(jnp.bfloat16)

    metric_copy.wait()
    ones = jnp.ones((8, fit), jnp.bfloat16)

    def prepare(k, carry):
        place(rows[0, pl.ds(k, 1), :], st_own.at[k])
        ms[k] = lax.dot_general(
            metric[k], st_own[k], NT, preferred_element_type=jnp.float32
        ).astype(jnp.bfloat16)
        mask[k] = lax.dot_general(ones, st_own[k], NT, preferred_element_type=jnp.float32)
        return carry

    lax.fori_loop(0, occ, prepare, 0)
    own_raw.wait()

    def lanes(l, step):
        return pl.ds(pl.multiple_of((l * n_orb + step) * osv, osv), osv)

    def fit_own(k, carry):
        def arrived(step, inner):
            raw_copy(k, step).wait_recv()
            return inner

        lax.fori_loop(1, n_aux, arrived, 0)
        dense = raw_full[k].reshape(aux_total, osv)
        block = jnp.dot(ms[k], dense, preferred_element_type=jnp.float32).astype(jnp.bfloat16)
        fitted[k, 0] = block
        for step in range(1, n_orb):
            fit_copy(k, step).start()
        rt[pl.ds(pl.multiple_of(k * osv, osv), osv), :] = jnp.where(
            mask[k, 0:1, :] > 0.5, dense.astype(jnp.float32).T, 0.0
        ).astype(jnp.bfloat16)
        grid_full[:, lanes(k, 0)] = jnp.dot(
            st_own[k], block, preferred_element_type=jnp.float32
        ).astype(jnp.bfloat16)
        return carry

    lax.fori_loop(0, occ, fit_own, 0)

    for step in range(1, n_orb):
        meta_copy(0, rows, step).wait_recv()
        meta_copy(1, levels, step).wait_recv()

    def partners(l, carry):
        def spread(step, inner):
            place(rows[step, pl.ds(l, 1), :], st_far)
            fit_copy(l, step).wait_recv()
            grid_full[:, lanes(l, step)] = jnp.dot(
                st_far[...], fitted[l, step], preferred_element_type=jnp.float32
            ).astype(jnp.bfloat16)
            return inner

        lax.fori_loop(1, n_orb, spread, 0)
        wide = n_orb * osv
        part = pl.ds(pl.multiple_of(l * wide, wide), wide)
        integrals[...] = jnp.dot(rt[...], grid_full[:, part], preferred_element_type=jnp.float32)

        def terms(step, inner):
            far = levels[step, pl.ds(l, 1), :]
            peer = lax.rem(my_orb - step + n_orb, n_orb)
            local = pl.ds(pl.multiple_of(step * osv, osv), osv)
            for k in range(occ):
                base = k * (matches + 1) * occ
                weight = jnp.where(step == 0, screen_ref[base + l], 0)
                for q in range(matches):
                    weight = weight + jnp.where(
                        jnp.logical_and(step > 0, match_ref[q * n_orb + my_orb] == peer),
                        screen_ref[base + (q + 1) * occ + l],
                        0,
                    )
                value = integrals[k * osv : (k + 1) * osv, local]
                bottom = level_col[k * osv : (k + 1) * osv, :] + far
                amp = (value / bottom).astype(jnp.bfloat16).astype(jnp.float32)
                energy_ref[l, step, k : k + 1, :] = jnp.sum(amp * value, axis=0, keepdims=True)
                amps[k * osv : (k + 1) * osv, lanes(l, step)] = (
                    amp * weight.astype(jnp.float32)
                ).astype(jnp.bfloat16)
            return inner

        return lax.fori_loop(0, n_orb, terms, carry)

    lax.fori_loop(0, occ, partners, 0)

    pair = 2
    my_pair = me // pair

    def density(which):
        height = pair * aux_dev
        part = grid_full[pl.ds(pl.multiple_of(which * height, height), height), :]
        found = lax.dot_general(part, amps[...], NT, preferred_element_type=jnp.float32)
        found = found.astype(jnp.bfloat16)
        for c in range(pair):
            for k in range(occ):
                outgoing[which * pair + c, k] = found[
                    c * aux_dev : (c + 1) * aux_dev, k * osv : (k + 1) * osv
                ]

    def far_density(step, carry):
        which = lax.rem(my_pair + step, n_aux // pair)
        density(which)
        for c in range(pair):
            den_copy(which * pair + c).start()
        return carry

    lax.fori_loop(1, n_aux // pair, far_density, 0)
    density(my_pair)
    buddy = my_pair * pair + 1 - lax.rem(me, pair)
    den_copy(buddy).start()
    own_out = pltpu.make_async_copy(outgoing.at[me], out_ref.at[me], local_sem.at[2])
    own_out.start()

    def drain_raw(k, carry):
        def one(step, inner):
            raw_copy(k, step).wait_send()
            return inner

        lax.fori_loop(1, n_aux, one, 0)

        def two(step, inner):
            fit_copy(k, step).wait_send()
            return inner

        return lax.fori_loop(1, n_orb, two, carry)

    lax.fori_loop(0, occ, drain_raw, 0)
    for step in range(1, n_orb):
        meta_copy(0, rows, step).wait_send()
        meta_copy(1, levels, step).wait_send()

    def drain_density(step, carry):
        copy = den_copy(aux_peer(step))
        copy.wait_send()
        copy.wait_recv()
        return carry

    lax.fori_loop(1, n_aux, drain_density, 0)
    own_out.wait()


def per_device(
    raw_rows, fit_metric, domain, counts, orbital_ids, occ_energy, osv_energy, matchings, screening
):
    n_aux = lax.axis_size("aux")
    n_orb = lax.axis_size("orb")
    my_orb = lax.axis_index("orb")
    group_slots, aux_dev, osv = raw_rows.shape
    occ = group_slots // n_aux
    fit = domain.shape[1]
    aux_total = aux_dev * n_aux
    matches = matchings.shape[0]
    bf16, f32 = jnp.bfloat16, jnp.float32
    anywhere = pl.BlockSpec(memory_space=pl.ANY)
    vmem = pl.BlockSpec(memory_space=pltpu.VMEM)
    smem = pl.BlockSpec(memory_space=pltpu.SMEM)
    dma = pltpu.SemaphoreType.DMA
    returned, sums = pl.pallas_call(
        functools.partial(kernel, n_orb, n_aux),
        out_shape=(
            jax.ShapeDtypeStruct((n_aux, occ, aux_dev, osv), bf16),
            jax.ShapeDtypeStruct((occ, n_orb, occ, osv), f32),
        ),
        in_specs=[anywhere, anywhere, vmem, smem, smem, smem, vmem, smem, smem],
        out_specs=(anywhere, vmem),
        scratch_shapes=[
            pltpu.VMEM((occ, n_aux, aux_dev, osv), bf16),
            pltpu.VMEM((occ, fit, fit), bf16),
            pltpu.VMEM((occ, aux_total, fit), bf16),
            pltpu.VMEM((aux_total, fit), bf16),
            pltpu.VMEM((occ, fit, aux_total), bf16),
            pltpu.VMEM((occ, 8, aux_total), f32),
            pltpu.VMEM((occ * osv, aux_total), bf16),
            pltpu.VMEM((occ, n_orb, fit, osv), bf16),
            pltpu.VMEM((n_orb, occ, fit), jnp.int32),
            pltpu.VMEM((n_orb, occ, osv), f32),
            pltpu.VMEM((occ * osv, osv), f32),
            pltpu.VMEM((aux_total, occ * n_orb * osv), bf16),
            pltpu.VMEM((occ * osv, n_orb * osv), f32),
            pltpu.VMEM((occ * osv, occ * n_orb * osv), bf16),
            pltpu.VMEM((n_aux, occ, aux_dev, osv), bf16),
            dma((occ, n_aux)),
            dma((occ, n_aux)),
            dma((occ, n_orb)),
            dma((occ, n_orb)),
            dma((2, n_orb)),
            dma((2, n_orb)),
            dma((n_aux,)),
            dma((n_aux,)),
            dma((3,)),
        ],
        compiler_params=pltpu.CompilerParams(
            collective_id=0, has_side_effects=True, vmem_limit_bytes=60 * 1024 * 1024
        ),
    )(
        raw_rows.reshape(n_aux, occ, aux_dev, osv),
        fit_metric,
        domain.reshape(n_aux, occ, fit),
        counts.reshape(-1),
        orbital_ids,
        occ_energy,
        osv_energy,
        matchings.reshape(-1),
        screening.reshape(-1),
    )
    density = returned.reshape(group_slots, aux_dev, osv).astype(f32)
    sums = jnp.sum(sums, axis=3)
    partner = lax.dynamic_index_in_dim(matchings, my_orb, 1, keepdims=False)
    step = jnp.concatenate([jnp.zeros((1,), jnp.int32), lax.rem(my_orb - partner + n_orb, n_orb)])
    chosen = step[:, None] == jnp.arange(n_orb, dtype=jnp.int32)[None, :]
    picked = jnp.sum(
        jnp.where(chosen[None, :, None, :], sums.transpose(2, 0, 1)[:, None, :, :], 0.0), axis=3
    )
    energy = PAIR_SCALE * screening.astype(f32) * picked / (osv * osv)
    return (density, energy)


def solution(mesh):
    placed = (
        P("orb", "aux", None),
        P(("orb", "aux"), None, None),
        P("orb", None),
        P("orb", None),
        P(("orb", "aux")),
        P(),
        P(("orb", "aux"), None),
        P(),
        P(("orb", "aux"), None, None),
    )
    return jax.shard_map(
        per_device,
        mesh=mesh,
        in_specs=placed,
        out_specs=(P("orb", "aux", None), P(("orb", "aux"), None, None)),
        check_vma=False,
    )
```

time: 278 us -> 83.4 us (0.30); the launches traced: 273 us -> 82.9 us
  local copies, waits for them, and re-layouts: 124 us -> 5.79 us
  Pallas kernels: 0 us -> 71.1 us
  waiting for transfers between devices: 52.4 us -> 0 us
  matrix products: 22.7 us -> 0 us
  between operations: 22.8 us -> 0.67 us
  blocking collectives: 17.8 us -> 0 us
  starting transfers between devices: 17.2 us -> 0 us
  other arithmetic: 16.7 us -> 5.32 us
    pallas_call x0 -> x1, Pallas kernels: none -> 71.1 us  [per_device(): pl.pallas_call(functools.partial(kernel, n_orb, n_aux), out_shape=(jax.Sh...]
    gather x6 -> x0, local copies, waits for them, and re-layouts: 64.8 us -> none  [the longest x1 32.8 us: per_device(): jnp.take_along_axis(domain, where_at, axis=1)]
    all_to_all x2 -> x0, waiting for transfers between devices: 52.4 us -> none  [the longest x1 37.9 us: per_device(): lax.all_to_all(density, 'aux', split_axis=1, concat_axis=0, tiled=True)]
    unnamed x74 -> x4, local copies, waits for them, and re-layouts: 46.9 us -> 1.57 us
    dot_general x11 -> x0, matrix products: 22.7 us -> none  [the longest x5 16.9 us: pair_terms(): jnp.einsum('kpa,lpb->klab', raw_full, spread_out, preferred_element_type=...]
    all_to_all x2 -> x0, starting transfers between devices: 17.2 us -> none  [the longest x1 11.9 us: per_device(): lax.all_to_all(density, 'aux', split_axis=1, concat_axis=0, tiled=True)]
    all_gather x2 -> x0, blocking collectives: 12.4 us -> none  [the longest x1 6.46 us: per_device(): lax.all_gather(rows_global, 'orb', axis=0, tiled=True)]
    reduce_sum x7 -> x2, other arithmetic: 7.72 us -> 0.96 us  [the longest x1 0.85 us: per_device(): sums = jnp.sum(sums, axis=3)]
  transfers between devices with their start and end apart: 3 -> 0, of which waited for: 2 -> 0; matrix products, arithmetic and copies ran while one was open for 14% -> 0% of each run, Pallas kernels for 0% -> 0%
where the time goes in v1:
time: 83.4 us; the launch traced here: 82.9 us
  Pallas kernels  71.1 us (85%)
  local copies, waits for them, and re-layouts  5.79 us (7%)
  other arithmetic  5.32 us (6%)
    pallas_call x1, Pallas kernels, per_device(): pl.pallas_call(functools.partial(kernel, n_orb, n_aux), out_shape=(jax.Sh...  71.1 us
    convert_element_type x1, other arithmetic, per_device(): density = returned.reshape(group_slots, aux_dev, osv).astype(f32)  2.79 us

profile of v1, /device:TPU:25, one launch (start us, length us, event | category | flops | bytes accessed | tf_op | source)
XLA Modules:
  0.0 82.9 jit_solution(6445028071651156501)
XLA Ops:
  0.6 0.0 copy-start
  0.6 0.9 %add_reduce_fusion = s32[4]{0:T(128)S(1)} fusion(s32[4,4]{1,0:T(4,128)} %param.16, s32[]{:T(128)S(6)} %select_n.8, s32[]{:T(128)S(6)} %axis_index.15), kind=kLoop, calls=%fused_computation.6 | loop fusion | flops 8 | bytes 40 | tf_op jit(solution)/shard_map/add | solution.py:356
  1.5 0.1 pad_add_fusion
  1.6 1.3 %reshape.48.match_ref = s32[16]{0:T(128)} reshape(s32[4,4]{1,0:T(4,128)} %param.16) | data formatting | bytes 128 | tf_op jit(solution)/shard_map/reshape | solution.py:350
  2.9 0.8 copy.17
  3.7 0.7 reshape.47.counts_ref
  4.3 0.8 copy.18
  5.1 0.7 reshape.49.screen_ref
  5.8 1.5 %reshape.46.domain_ref = s32[8,4,512]{2,1,0:T(4,128)} reshape(s32[32,512]{1,0:T(8,128)} %param.11) | data formatting | bytes 131072 | tf_op jit(solution)/shard_map/reshape | solution.py:345
  7.3 71.1 %shard_map.104 = (bf16[8,4,128,128]{3,2,1,0:T(8,128)(2,1)}, f32[4,4,4,128]{3,2,1,0:T(4,128)}) custom-call(bf16[8,4,128,128]{3,2,1,0:T(8,128)(2,1)} %bitcast.5, bf16[4,512,512]{2,1,0:T(8,128)(2,1)} %metric_ref.1, s32[8,4,512]{2,1,0:T(4,128)} %reshape.46.domain_ref, s32[256]{0:T(256)} %reshape.47.counts_ref, s32[4]{0:T(128)} %ids_ref.1, f32[128]{0:T(128)} %occ_ref.1, ...), custom_call_target="tpu_custom_call" | custom-call | tf_op jit(solution)/shard_map/pallas_call | solution.py:305
  78.4 0.9 %reduce_sum.18 = f32[4,4,4]{2,1,0:T(4,128)S(1)} reduce(f32[4,4,4,128]{3,2,1,0:T(4,128)} %get-tuple-element.5, f32[]{:T(128)} %constant.22.clone.1), dimensions={3}, to_apply=%region_0.0 | reduce | flops 8128 | bytes 33028 | tf_op jit(solution)/shard_map/reduce_sum | solution.py:354
  79.3 0.1 copy.19
  79.4 0.1 select_reduce_fusion
  79.5 0.0 copy-done
  79.5 0.6 multiply_multiply_fusion
  80.1 2.8 %bitcast_convert_fusion = f32[32,128,128]{2,1,0:T(8,128)} fusion(bf16[8,4,128,128]{3,2,1,0:T(8,128)(2,1)} %get-tuple-element.4), kind=kLoop, calls=%fused_computation | loop fusion | flops 524288 | bytes 3145728 | tf_op jit(solution)/shard_map/convert_element_type | solution.py:353
  (2 shorter events, 0.0 us)
Async XLA Ops:
  0.6 78.9 %copy-start = (s32[4,5,4]{1,2,0:T(4,128)S(1)}, s32[4,5,4]{1,2,0:T(4,128)}, u32[]{:S(2)}) copy-start(s32[4,5,4]{1,2,0:T(4,128)} %param.17) | copy-start | bytes 964

commit v2 on v1

--- a/solution.py
+++ b/solution.py
@@ -31,7 +31,6 @@
     st_own,
     st_far,
     ms,
-    mask,
     rt,
     fitted,
     rows,
@@ -41,6 +40,8 @@
     integrals,
     amps,
     outgoing,
+    sums,
+    totals,
     raw_send,
     raw_recv,
     fit_send,
@@ -54,7 +55,7 @@
     occ, fit = metric_ref.shape[0], metric_ref.shape[1]
     aux_dev, osv = raw_ref.shape[2], raw_ref.shape[3]
     aux_total = n_aux * aux_dev
-    matches = match_ref.shape[0] // n_orb
+    matches = match_ref.shape[0]
     my_orb = lax.axis_index("orb")
     me = lax.axis_index("aux")
 
@@ -70,10 +71,15 @@
     for step in range(1, n_orb):
         pl.semaphore_signal(barrier, inc=1, device_id=(orb_peer(step), me), device_id_type=MESH)
 
-    metric_copy = pltpu.make_async_copy(metric_ref, metric, local_sem.at[0])
-    metric_copy.start()
-    own_raw = pltpu.make_async_copy(raw_ref.at[me], raw_full.at[:, me], local_sem.at[1])
-    own_raw.start()
+    def metric_copy(k):
+        return pltpu.make_async_copy(metric_ref.at[k], metric.at[k], local_sem.at[0, k])
+
+    def own_raw(k):
+        return pltpu.make_async_copy(raw_ref.at[me, k], raw_full.at[k, me], local_sem.at[1, k])
+
+    for k in range(occ):
+        metric_copy(k).start()
+        own_raw(k).start()
     pl.semaphore_wait(barrier, n_aux + n_orb - 2)
 
     def raw_copy(k, step):
@@ -130,9 +136,9 @@
         end = jnp.int32(0)
         owner = jnp.zeros((1, fit), jnp.int32)
         for j in range(n_aux):
-            end = end + counts_ref[(me * occ + k) * n_aux + j]
+            end = end + counts_ref[j, me * occ + k]
             owner = owner + jnp.where(positions >= end, 1, 0)
-        rows[0, k : k + 1, :] = owner * aux_dev + domain_ref[me, k : k + 1, :]
+        rows[0, k : k + 1, :] = owner * aux_dev + domain_ref[pl.ds(me * occ + k, 1), :]
         level = osv_ref[k : k + 1, :].astype(jnp.float32) - occ_ref[ids_ref[k]]
         levels[0, k : k + 1, :] = level
         level_col[k * osv : (k + 1) * osv, :] = jnp.broadcast_to(level, (osv, osv)).T
@@ -142,64 +148,81 @@
 
     def place(row, target):
         height = 128
-        base = lax.broadcasted_iota(jnp.int32, (height, fit), 0)
+        base = lax.broadcasted_iota(jnp.int32, (height, fit), 0).astype(jnp.bfloat16)
+        one, zero = jnp.ones((), jnp.bfloat16), jnp.zeros((), jnp.bfloat16)
         for j in range(aux_total // height):
-            target[j * height : (j + 1) * height, :] = jnp.where(
-                base == row - j * height, 1.0, 0.0
-            ).astype(jnp.bfloat16)
-
-    metric_copy.wait()
-    ones = jnp.ones((8, fit), jnp.bfloat16)
-
-    def prepare(k, carry):
-        place(rows[0, pl.ds(k, 1), :], st_own.at[k])
-        ms[k] = lax.dot_general(
-            metric[k], st_own[k], NT, preferred_element_type=jnp.float32
-        ).astype(jnp.bfloat16)
-        mask[k] = lax.dot_general(ones, st_own[k], NT, preferred_element_type=jnp.float32)
-        return carry
-
-    lax.fori_loop(0, occ, prepare, 0)
-    own_raw.wait()
+            inside = jnp.logical_and(row >= j * height, row < (j + 1) * height)
+            wanted = jnp.where(inside, row - j * height, -1).astype(jnp.bfloat16)
+            target[j * height : (j + 1) * height, :] = jnp.where(base == wanted, one, zero)
 
     def lanes(l, step):
         return pl.ds(pl.multiple_of((l * n_orb + step) * osv, osv), osv)
 
+    ones = jnp.ones((8, fit), jnp.bfloat16)
+
+    def place_far(l):
+        def one(step, inner):
+            place(rows[step, pl.ds(l, 1), :], st_far.at[step - 1])
+            return inner
+
+        lax.fori_loop(1, n_orb, one, 0)
+
+    def spread_far(l):
+        def one(step, inner):
+            fit_copy(l, step).wait_recv()
+            grid_full[:, lanes(l, step)] = jnp.dot(
+                st_far[step - 1], fitted[l, step], preferred_element_type=jnp.float32
+            ).astype(jnp.bfloat16)
+            return inner
+
+        lax.fori_loop(1, n_orb, one, 0)
+
     def fit_own(k, carry):
+        place(rows[0, pl.ds(k, 1), :], st_own)
+        metric_copy(k).wait()
+        ms[...] = lax.dot_general(
+            metric[k], st_own[...], NT, preferred_element_type=jnp.float32
+        ).astype(jnp.bfloat16)
+        mask = lax.dot_general(ones, st_own[...], NT, preferred_element_type=jnp.float32)
+
         def arrived(step, inner):
             raw_copy(k, step).wait_recv()
             return inner
 
         lax.fori_loop(1, n_aux, arrived, 0)
+        own_raw(k).wait()
         dense = raw_full[k].reshape(aux_total, osv)
-        block = jnp.dot(ms[k], dense, preferred_element_type=jnp.float32).astype(jnp.bfloat16)
+        block = jnp.dot(ms[...], dense, preferred_element_type=jnp.float32).astype(jnp.bfloat16)
         fitted[k, 0] = block
         for step in range(1, n_orb):
             fit_copy(k, step).start()
         rt[pl.ds(pl.multiple_of(k * osv, osv), osv), :] = jnp.where(
-            mask[k, 0:1, :] > 0.5, dense.astype(jnp.float32).T, 0.0
+            mask[0:1, :] > 0.5, dense.astype(jnp.float32).T, 0.0
         ).astype(jnp.bfloat16)
         grid_full[:, lanes(k, 0)] = jnp.dot(
-            st_own[k], block, preferred_element_type=jnp.float32
+            st_own[...], block, preferred_element_type=jnp.float32
         ).astype(jnp.bfloat16)
+
+        @pl.when(k == 0)
+        def _():
+            for step in range(1, n_orb):
+                meta_copy(0, rows, step).wait_recv()
+                meta_copy(1, levels, step).wait_recv()
+
+        @pl.when(k > 0)
+        def _():
+            spread_far(k - 1)
+
+        place_far(k)
         return carry
 
     lax.fori_loop(0, occ, fit_own, 0)
 
-    for step in range(1, n_orb):
-        meta_copy(0, rows, step).wait_recv()
-        meta_copy(1, levels, step).wait_recv()
-
     def partners(l, carry):
-        def spread(step, inner):
-            place(rows[step, pl.ds(l, 1), :], st_far)
-            fit_copy(l, step).wait_recv()
-            grid_full[:, lanes(l, step)] = jnp.dot(
-                st_far[...], fitted[l, step], preferred_element_type=jnp.float32
-            ).astype(jnp.bfloat16)
-            return inner
-
-        lax.fori_loop(1, n_orb, spread, 0)
+        @pl.when(l == occ - 1)
+        def _():
+            spread_far(l)
+
         wide = n_orb * osv
         part = pl.ds(pl.multiple_of(l * wide, wide), wide)
         integrals[...] = jnp.dot(rt[...], grid_full[:, part], preferred_element_type=jnp.float32)
@@ -209,18 +232,17 @@
             peer = lax.rem(my_orb - step + n_orb, n_orb)
             local = pl.ds(pl.multiple_of(step * osv, osv), osv)
             for k in range(occ):
-                base = k * (matches + 1) * occ
-                weight = jnp.where(step == 0, screen_ref[base + l], 0)
+                weight = jnp.where(step == 0, screen_ref[k, l, 0], 0)
                 for q in range(matches):
                     weight = weight + jnp.where(
-                        jnp.logical_and(step > 0, match_ref[q * n_orb + my_orb] == peer),
-                        screen_ref[base + (q + 1) * occ + l],
+                        jnp.logical_and(step > 0, match_ref[q, my_orb] == peer),
+                        screen_ref[k, l, q + 1],
                         0,
                     )
                 value = integrals[k * osv : (k + 1) * osv, local]
                 bottom = level_col[k * osv : (k + 1) * osv, :] + far
                 amp = (value / bottom).astype(jnp.bfloat16).astype(jnp.float32)
-                energy_ref[l, step, k : k + 1, :] = jnp.sum(amp * value, axis=0, keepdims=True)
+                sums[l, step, k : k + 1, :] = jnp.sum(amp * value, axis=0, keepdims=True)
                 amps[k * osv : (k + 1) * osv, lanes(l, step)] = (
                     amp * weight.astype(jnp.float32)
                 ).astype(jnp.bfloat16)
@@ -255,8 +277,23 @@
     density(my_pair)
     buddy = my_pair * pair + 1 - lax.rem(me, pair)
     den_copy(buddy).start()
-    own_out = pltpu.make_async_copy(outgoing.at[me], out_ref.at[me], local_sem.at[2])
+    own_out = pltpu.make_async_copy(outgoing.at[me], out_ref.at[me], local_sem.at[2, 0])
     own_out.start()
+
+    def energies(l, carry):
+        for k in range(occ):
+            for step in range(n_orb):
+                totals[step] = jnp.sum(sums[l, step, k : k + 1, :]) * (PAIR_SCALE / (osv * osv))
+            energy_ref[k, l, 0] = screen_ref[k, l, 0].astype(jnp.float32) * totals[0]
+            for q in range(matches):
+                found = jnp.float32(0.0)
+                for step in range(1, n_orb):
+                    peer = lax.rem(my_orb - step + n_orb, n_orb)
+                    found = jnp.where(match_ref[q, my_orb] == peer, totals[step], found)
+                energy_ref[k, l, q + 1] = screen_ref[k, l, q + 1].astype(jnp.float32) * found
+        return carry
+
+    lax.fori_loop(0, occ, energies, 0)
 
     def drain_raw(k, carry):
         def one(step, inner):
@@ -291,32 +328,29 @@
 ):
     n_aux = lax.axis_size("aux")
     n_orb = lax.axis_size("orb")
-    my_orb = lax.axis_index("orb")
     group_slots, aux_dev, osv = raw_rows.shape
     occ = group_slots // n_aux
     fit = domain.shape[1]
     aux_total = aux_dev * n_aux
-    matches = matchings.shape[0]
     bf16, f32 = jnp.bfloat16, jnp.float32
     anywhere = pl.BlockSpec(memory_space=pl.ANY)
     vmem = pl.BlockSpec(memory_space=pltpu.VMEM)
     smem = pl.BlockSpec(memory_space=pltpu.SMEM)
     dma = pltpu.SemaphoreType.DMA
-    returned, sums = pl.pallas_call(
+    returned, energy = pl.pallas_call(
         functools.partial(kernel, n_orb, n_aux),
         out_shape=(
             jax.ShapeDtypeStruct((n_aux, occ, aux_dev, osv), bf16),
-            jax.ShapeDtypeStruct((occ, n_orb, occ, osv), f32),
+            jax.ShapeDtypeStruct((occ, occ, screening.shape[1]), f32),
         ),
         in_specs=[anywhere, anywhere, vmem, smem, smem, smem, vmem, smem, smem],
-        out_specs=(anywhere, vmem),
+        out_specs=(anywhere, smem),
         scratch_shapes=[
             pltpu.VMEM((occ, n_aux, aux_dev, osv), bf16),
             pltpu.VMEM((occ, fit, fit), bf16),
-            pltpu.VMEM((occ, aux_total, fit), bf16),
             pltpu.VMEM((aux_total, fit), bf16),
-            pltpu.VMEM((occ, fit, aux_total), bf16),
-            pltpu.VMEM((occ, 8, aux_total), f32),
+            pltpu.VMEM((n_orb - 1, aux_total, fit), bf16),
+            pltpu.VMEM((fit, aux_total), bf16),
             pltpu.VMEM((occ * osv, aux_total), bf16),
             pltpu.VMEM((occ, n_orb, fit, osv), bf16),
             pltpu.VMEM((n_orb, occ, fit), jnp.int32),
@@ -326,6 +360,8 @@
             pltpu.VMEM((occ * osv, n_orb * osv), f32),
             pltpu.VMEM((occ * osv, occ * n_orb * osv), bf16),
             pltpu.VMEM((n_aux, occ, aux_dev, osv), bf16),
+            pltpu.VMEM((occ, n_orb, occ, osv), f32),
+            pltpu.SMEM((n_orb,), f32),
             dma((occ, n_aux)),
             dma((occ, n_aux)),
             dma((occ, n_orb)),
@@ -334,32 +370,24 @@
             dma((2, n_orb)),
             dma((n_aux,)),
             dma((n_aux,)),
-            dma((3,)),
+            dma((3, occ)),
         ],
         compiler_params=pltpu.CompilerParams(
-            collective_id=0, has_side_effects=True, vmem_limit_bytes=60 * 1024 * 1024
+            collective_id=0, has_side_effects=True, vmem_limit_bytes=56 * 1024 * 1024
         ),
     )(
         raw_rows.reshape(n_aux, occ, aux_dev, osv),
         fit_metric,
-        domain.reshape(n_aux, occ, fit),
-        counts.reshape(-1),
+        domain,
+        counts.T,
         orbital_ids,
         occ_energy,
         osv_energy,
-        matchings.reshape(-1),
-        screening.reshape(-1),
+        matchings,
+        screening.transpose(0, 2, 1),
     )
     density = returned.reshape(group_slots, aux_dev, osv).astype(f32)
-    sums = jnp.sum(sums, axis=3)
-    partner = lax.dynamic_index_in_dim(matchings, my_orb, 1, keepdims=False)
-    step = jnp.concatenate([jnp.zeros((1,), jnp.int32), lax.rem(my_orb - partner + n_orb, n_orb)])
-    chosen = step[:, None] == jnp.arange(n_orb, dtype=jnp.int32)[None, :]
-    picked = jnp.sum(
-        jnp.where(chosen[None, :, None, :], sums.transpose(2, 0, 1)[:, None, :, :], 0.0), axis=3
-    )
-    energy = PAIR_SCALE * screening.astype(f32) * picked / (osv * osv)
-    return (density, energy)
+    return (density, energy.transpose(0, 2, 1))
 
 
 def solution(mesh):

time: 83.4 us -> 75.3 us (0.903)
  local copies, waits for them, and re-layouts: 5.79 us -> 0.6 us
  other arithmetic: 5.32 us -> 2.79 us
    reshape x4 -> x0, local copies, waits for them, and re-layouts: 4.11 us -> none  [the longest x1 1.49 us: per_device(): domain.reshape(n_aux, occ, fit)]
    unnamed x4 -> x3, local copies, waits for them, and re-layouts: 1.57 us -> 0.6 us
    reduce_sum x2 -> x0, other arithmetic: 0.96 us -> none  [the longest x1 0.85 us: per_device(): sums = jnp.sum(sums, axis=3)]
    add x1 -> x0, other arithmetic: 0.87 us -> none  [per_device(): my_orb - partner + n_orb]
where the time goes in v2:
time: 75.3 us; the launch traced here: 75 us
  Pallas kernels  70.9 us (94%)
  other arithmetic  2.79 us (4%)
    pallas_call x1, Pallas kernels, per_device(): pl.pallas_call(functools.partial(kernel, n_orb, n_aux), out_shape=(jax.Sh...  70.9 us
    convert_element_type x1, other arithmetic, per_device(): density = returned.reshape(group_slots, aux_dev, osv).astype(f32)  2.79 us

profile of v2, /device:TPU:25, one launch (start us, length us, event | category | flops | bytes accessed | tf_op | source)
XLA Modules:
  0.0 75.0 jit_solution(1065191040820450537)
XLA Ops:
  0.6 70.9 %shard_map.104 = (bf16[8,4,128,128]{3,2,1,0:T(8,128)(2,1)}, f32[4,4,5]{2,1,0:T(4,128)}) custom-call(bf16[8,4,128,128]{3,2,1,0:T(8,128)(2,1)} %bitcast.7, bf16[4,512,512]{2,1,0:T(8,128)(2,1)} %metric_ref.1, s32[32,512]{1,0:T(8,128)} %domain_ref.1, s32[8,32]{1,0:T(8,128)} %bitcast.10, s32[4]{0:T(128)} %ids_ref.1, f32[128]{0:T(128)} %occ_ref.1, ...), custom_call_target="tpu_custom_call" | custom-call | tf_op jit(solution)/shard_map/pallas_call | solution.py:340
  71.6 0.0 copy-start
  71.6 2.8 %bitcast_convert_fusion = f32[32,128,128]{2,1,0:T(8,128)} fusion(bf16[8,4,128,128]{3,2,1,0:T(8,128)(2,1)} %get-tuple-element.4), kind=kLoop, calls=%fused_computation | loop fusion | flops 524288 | bytes 3145728 | tf_op jit(solution)/shard_map/convert_element_type | solution.py:389
  74.4 0.0 copy-done
  74.4 0.6 copy.12
Async XLA Ops:
  71.6 2.8 %copy-start = (f32[4,4,5]{2,1,0:T(4,128)S(1)}, f32[4,4,5]{2,1,0:T(4,128)}, u32[]{:S(2)}) copy-start(f32[4,4,5]{2,1,0:T(4,128)} %get-tuple-element.5) | copy-start | bytes 964

commit v3 on v2

--- a/solution.py
+++ b/solution.py
@@ -267,7 +267,7 @@
                 ]
 
     def far_density(step, carry):
-        which = lax.rem(my_pair + step, n_aux // pair)
+        which = lax.rem(my_pair + n_aux // pair - step, n_aux // pair)
         density(which)
         for c in range(pair):
             den_copy(which * pair + c).start()

time: 75.3 us -> 74.2 us (0.985)
  the two profiles are of different devices: /device:TPU:25 before, /device:TPU:1 now
where the time goes in v3:
time: 74.2 us; the launch traced here: 74 us
  Pallas kernels  69.9 us (94%)
  other arithmetic  2.79 us (4%)
    pallas_call x1, Pallas kernels, per_device(): pl.pallas_call(functools.partial(kernel, n_orb, n_aux), out_shape=(jax.Sh...  69.9 us
    convert_element_type x1, other arithmetic, per_device(): density = returned.reshape(group_slots, aux_dev, osv).astype(f32)  2.79 us

profile of v3, /device:TPU:1, one launch (start us, length us, event | category | flops | bytes accessed | tf_op | source)
XLA Modules:
  0.0 74.0 jit_solution(3222759072364704839)
XLA Ops:
  0.6 69.9 %shard_map.104 = (bf16[8,4,128,128]{3,2,1,0:T(8,128)(2,1)}, f32[4,4,5]{2,1,0:T(4,128)}) custom-call(bf16[8,4,128,128]{3,2,1,0:T(8,128)(2,1)} %bitcast.7, bf16[4,512,512]{2,1,0:T(8,128)(2,1)} %metric_ref.1, s32[32,512]{1,0:T(8,128)} %domain_ref.1, s32[8,32]{1,0:T(8,128)} %bitcast.10, s32[4]{0:T(128)} %ids_ref.1, f32[128]{0:T(128)} %occ_ref.1, ...), custom_call_target="tpu_custom_call" | custom-call | tf_op jit(solution)/shard_map/pallas_call | solution.py:340
  70.6 0.0 copy-start
  70.6 2.8 %bitcast_convert_fusion = f32[32,128,128]{2,1,0:T(8,128)} fusion(bf16[8,4,128,128]{3,2,1,0:T(8,128)(2,1)} %get-tuple-element.4), kind=kLoop, calls=%fused_computation | loop fusion | flops 524288 | bytes 3145728 | tf_op jit(solution)/shard_map/convert_element_type | solution.py:389
  73.4 0.0 copy-done
  73.4 0.6 copy.12
Async XLA Ops:
  70.6 2.8 %copy-start = (f32[4,4,5]{2,1,0:T(4,128)S(1)}, f32[4,4,5]{2,1,0:T(4,128)}, u32[]{:S(2)}) copy-start(f32[4,4,5]{2,1,0:T(4,128)} %get-tuple-element.5) | copy-start | bytes 964
